TPU v7x, 32 devices: a whole 2x2x4 slice. The times are simulated.
32 devices in a mesh: aux: 8 (over z, x), row: 4 (over y, core).
Axes of the slice: x: 2, y: 2, z: 4, core: 2. Of those that a mesh axis runs over, the one named last changes fastest.
Arguments:
- slabs: bfloat16 [64, 400, 2048], P('aux', None, 'row'), may hold values from -0.47265625 to 0.47265625
- significant: int32 [64, 32], P('aux'), may hold values from 0 to 1, as said below
Outputs:
- exchange: float32 [2048, 2048], P('row', 'aux')
Inputs may be any that keep to these rules, and one draw needn't show every extreme that they name: `significant`: each entry is 0 or 1; the share of ones differs between the auxiliary functions of different devices.
All inputs are finite; a program needn't handle non-finite values.
Results may differ from a plain program's by a relative error of at most 0.0003.
Values may be sent and summed in bfloat16 or wider, within the bound.
A program may use at most 64 MiB of HBM per device.

v0:
```python
import jax
import jax.numpy as jnp
from jax import lax
from jax.sharding import PartitionSpec as P

BS = 64


def local(slabs, significant):
    aux_here, occupied, rows_here = slabs.shape
    blocks_here = rows_here // BS
    first_block = lax.axis_index("row") * blocks_here
    local_mask = lax.dynamic_slice_in_dim(significant, first_block, blocks_here, 1).astype(
        jnp.float32
    )
    block_of = lax.broadcasted_iota(jnp.int32, (blocks_here, rows_here), 1) // BS
    block_id = lax.broadcasted_iota(jnp.int32, (blocks_here, rows_here), 0)
    expand_table = (block_of == block_id).astype(jnp.float32)
    column_mask = jnp.dot(local_mask, expand_table).astype(jnp.bfloat16)
    masked = (slabs * column_mask[:, None, :]).reshape(aux_here * occupied, rows_here)
    partial_rows = lax.dot_general(
        masked,
        lax.all_gather(masked, "row", axis=1, tiled=True),
        (((0,), (0,)), ((), ())),
        preferred_element_type=jnp.float32,
    )
    return lax.psum_scatter(partial_rows, "aux", scatter_dimension=1, tiled=True)


def solution(mesh):
    return jax.shard_map(
        local,
        mesh=mesh,
        in_specs=(P("aux", None, "row"), P("aux", None)),
        out_specs=P("row", "aux"),
        check_vma=False,
    )
```

profile of v0, /device:TPU:19, one launch (start us, length us, event | category | flops | bytes accessed | tf_op | source)
XLA Modules:
  0.0 204.4 jit_solution(1079189664257460225)
XLA Ops:
  6.5 0.0 all-gather.2.cloned.1.call-start
  6.6 0.9 convolution_convert_fusion
  7.4 3.8 %broadcast_multiply_fusion = bf16[8,400,512]{2,1,0:T(8,128)(2,1)} fusion(bf16[8,400,512]{2,1,0:T(8,128)(2,1)} %param.2, bf16[8,512]{1,0:T(8,128)(2,1)S(1)} %convolution_convert_fusion), kind=kLoop, calls=%fused_computation | loop fusion | flops 1638400 | bytes 6561792 | tf_op jit(solution)/shard_map/mul | solution.py:20
  11.3 0.0 copy-start
  11.3 0.0 all-gather.2.cloned.1.call-update
  11.3 0.0 reduce-scatter.2.cloned.1.call-start
  11.3 86.6 %all-gather.2.cloned.1.call-done = bf16[3200,2048]{1,0:T(8,128)(2,1)} async-done(((bf16[3200,512]{1,0:T(8,128)(2,1)}), bf16[3200,2048]{1,0:T(8,128)(2,1)}) %all-gather.2.cloned.1.call-update) | async-done | bytes 13107216 | tf_op jit(solution)/shard_map/all_gather | solution.py:23
  98.0 0.0 copy-done
  98.0 11.5 %fusion.9 = f32[512,2048]{1,0:T(8,128)} fusion(bf16[3200,512]{1,0:T(8,128)(2,1)S(1)} %bitcast.4, bf16[3200,2048]{1,0:T(8,128)(2,1)} %all-gather.2.cloned.1.call-done), kind=kOutput, calls=%fused_computation.16 | convolution fusion | flops 6710886400 | bytes 20578304 | tf_op jit(solution)/shard_map/dot_general | solution.py:21
  109.5 0.0 reduce-scatter.2.cloned.1.call-update
  109.5 88.0 %reduce-scatter.2.cloned.1.call-done = f32[512,256]{1,0:T(8,128)} async-done(((f32[512,2048]{1,0:T(8,128)}), f32[512,256]{1,0:T(8,128)}) %reduce-scatter.2.cloned.1.call-update) | async-done | bytes 524304 | tf_op jit(solution)/shard_map/reduce_scatter | solution.py:27
  (2 shorter events, 0.0 us)
Async XLA Ops:
  6.5 91.4 %all-gather.2.cloned.1.call-start = ((), (), s32[]{:S(2)}) async-start(), calls=%async_computation.1 | async-start | bytes 16384000 | tf_op jit(solution)/shard_map/all_gather | solution.py:23
  11.3 86.7 %copy-start = (bf16[8,400,512]{2,1,0:T(8,128)(2,1)S(1)}, bf16[8,400,512]{2,1,0:T(8,128)(2,1)}, u32[]{:S(2)}) copy-start(bf16[8,400,512]{2,1,0:T(8,128)(2,1)} %broadcast_multiply_fusion) | copy-start | bytes 9830404
  11.3 186.3 %reduce-scatter.2.cloned.1.call-start = ((), (), s32[]{:S(2)}) async-start(), calls=%async_computation.2 | async-start | bytes 4718592 | tf_op jit(solution)/shard_map/reduce_scatter | solution.py:27
Sparse Core Ops, SparseCore 0:
  11.4 86.5 all-gather.1
  109.6 87.8 reduce-scatter.1
where the time goes:
time: 207 us; the launch traced here: 204 us
  waiting for transfers between devices  175 us (85%)
  between operations  13.4 us (6%)
  matrix products  12.4 us (6%)
  other arithmetic  3.84 us (2%)
    reduce_scatter x1, waiting for transfers between devices, local(): lax.psum_scatter(partial_rows, 'aux', scatter_dimension=1, tiled=True)  88 us
    all_gather x1, waiting for transfers between devices, local(): lax.all_gather(masked, 'row', axis=1, tiled=True)  86.6 us
    dot_general x1, matrix products, local(): lax.dot_general(masked, lax.all_gather(masked, 'row', axis=1, tiled=True)...  11.5 us
  transfers between devices with their start and end apart: 2, of which 2 were waited for; matrix products, arithmetic and copies ran while one was open for 0% of the time, Pallas kernels for 0%

commit v1 on v0

--- a/solution.py
+++ b/solution.py
@@ -1,12 +1,19 @@
+import functools
+
 import jax
 import jax.numpy as jnp
 from jax import lax
+from jax.experimental import pallas as pl
+from jax.experimental.pallas import tpu as pltpu
 from jax.sharding import PartitionSpec as P
 
 BS = 64
-
-
-def local(slabs, significant):
+LANES = 128
+SUB = 128
+LAG = 3
+
+
+def plain(slabs, significant):
     aux_here, occupied, rows_here = slabs.shape
     blocks_here = rows_here // BS
     first_block = lax.axis_index("row") * blocks_here
@@ -27,7 +34,184 @@
     return lax.psum_scatter(partial_rows, "aux", scatter_dimension=1, tiled=True)
 
 
+def kernel(n_aux, n_row, occupied, slab_hbm, mask_ref, out_ref, g, lhs_t, mk, ps, xr, zb, zlo, zhi,
+           own_sem, psend, precv, ysend, yrecv, fsend, frecv, xsend, xrecv, zsend, zlo_sem, zhi_sem):
+    depth = slab_hbm.shape[0]
+    chunks = g.shape[1]
+    rows = ps.shape[3]
+    subs = rows // SUB
+    width = chunks * LANES
+    a, r = lax.axis_index("aux"), lax.axis_index("row")
+    z, x = a // 2, a % 2
+    last = n_aux // 2 - 1
+    y, c = r // 2, r % 2
+    partner = y * 2 + (1 - c)
+    across = (1 - y) * 2 + c
+    owner = (r, partner, across, (1 - y) * 2 + (1 - c))
+    beside = z * 2 + (1 - x)
+
+    barrier = pltpu.get_barrier_semaphore()
+    for there in ({"row": partner}, {"row": across}, {"aux": beside},
+                  {"aux": lax.rem(a + 2, n_aux)}, {"aux": lax.rem(a + n_aux - 2, n_aux)}):
+        pl.semaphore_signal(barrier, inc=1, device_id=there, device_id_type=pl.DeviceIdType.MESH)
+
+    def piece(j, h):
+        return slab_hbm.at[:, pl.ds(h * width + j * LANES, LANES)]
+
+    def remote(src, dst, send, recv, there):
+        return pltpu.make_async_remote_copy(
+            src_ref=src, dst_ref=dst, send_sem=send, recv_sem=recv, device_id=there,
+            device_id_type=pl.DeviceIdType.MESH,
+        )
+
+    both = [(j, h) for j in range(chunks) for h in range(2)]
+    own = {w: pltpu.make_async_copy(piece(*w), g.at[(0,) + w], own_sem.at[w]) for w in both}
+    for w in both:
+        own[w].start()
+    pl.semaphore_wait(barrier, 5)
+    to_y = {w: remote(piece(*w), g.at[(2,) + w], ysend.at[w], yrecv.at[w], {"row": across}) for w in both}
+    to_p = {w: remote(piece(*w), g.at[(1,) + w], psend.at[w], precv.at[w], {"row": partner}) for w in both}
+    fwd = {w: remote(g.at[(2,) + w], g.at[(3,) + w], fsend.at[w], frecv.at[w], {"row": partner}) for w in both}
+    for w in both:
+        to_y[w].start()
+    for w in both:
+        to_p[w].start()
+
+    def masked(k, j, h):
+        raw = g[k, j, h].reshape(-1, occupied // 16, 16, LANES)
+        return (raw * mask_ref[owner[k], h, j][:, None]).reshape(depth, LANES)
+
+    def x_copy(k, j, s):
+        part = pl.ds(s * SUB, SUB)
+        return remote(ps.at[k, j, 1 - x, part], xr.at[k, j, part], xsend.at[k, j, s], xrecv.at[k, j, s],
+                      {"aux": beside})
+
+    def z_copy(k, j, s, up):
+        part = pl.ds(s * SUB, SUB)
+        land, sem = (zlo, zlo_sem) if up else (zhi, zhi_sem)
+        return remote(zb.at[k, j, part], land.at[k, j, part], zsend.at[k, j, s], sem.at[k, j, s],
+                      {"aux": jnp.minimum(a + 2, n_aux - 1) if up else jnp.maximum(a - 2, 0)})
+
+    def multiply(k, j):
+        for h in range(2):
+            mk[:, h * LANES:(h + 1) * LANES] = masked(k, j, h)
+
+        @pl.loop(0, subs)
+        def _(s):
+            part = pl.ds(pl.multiple_of(s * SUB, SUB), SUB)
+            acc = jnp.dot(lhs_t[part, :], mk[...], preferred_element_type=jnp.float32)
+            ps[k, j, 0, part, :] = acc[:, :LANES]
+            ps[k, j, 1, part, :] = acc[:, LANES:]
+
+        for s in range(subs):
+            x_copy(k, j, s).start()
+
+    def sum_x(k, j, s):
+        d = owner[k]
+        part = pl.ds(s * SUB, SUB)
+        x_copy(k, j, s).wait_recv()
+        zb[k, j, part, :] = ps[k, j, x, part, :] + xr[k, j, part, :]
+        pl.when((z == 0) & (d > 0))(lambda: z_copy(k, j, s, True).start())
+        pl.when((z == last) & (d < last))(lambda: z_copy(k, j, s, False).start())
+
+    def sum_z(k, j, s):
+        d = owner[k]
+        part = pl.ds(s * SUB, SUB)
+
+        @pl.when((z > 0) & (z <= d))
+        def _():
+            z_copy(k, j, s, True).wait_recv()
+            zb[k, j, part, :] += zlo[k, j, part, :]
+
+        @pl.when((z < last) & (z >= d))
+        def _():
+            z_copy(k, j, s, False).wait_recv()
+            zb[k, j, part, :] += zhi[k, j, part, :]
+
+        pl.when((z > 0) & (z < d))(lambda: z_copy(k, j, s, True).start())
+        pl.when((z < last) & (z > d))(lambda: z_copy(k, j, s, False).start())
+
+        @pl.when(z == d)
+        def _():
+            out_ref[part, j * LANES:(j + 1) * LANES] = zb[k, j, part, :]
+
+    def reduce(jobs):
+        for t in range(len(jobs) + LAG):
+            if t < len(jobs):
+                sum_x(*jobs[t])
+            if t >= LAG:
+                sum_z(*jobs[t - LAG])
+
+    for j, h in both:
+        own[j, h].wait()
+        mk[:, :LANES] = masked(0, j, h)
+        lhs_t[h * width + j * LANES:h * width + (j + 1) * LANES, :] = mk[:, :LANES].T
+    for j in range(chunks):
+        multiply(0, j)
+    for j in range(chunks):
+        for h in range(2):
+            to_p[j, h].wait_recv()
+        multiply(1, j)
+    reduce([(k, j, s) for k in range(2) for j in range(chunks) for s in range(subs)])
+    for j in range(chunks):
+        for h in range(2):
+            to_y[j, h].wait_recv()
+            fwd[j, h].start()
+        multiply(2, j)
+        for h in range(2):
+            fwd[j, h].wait_recv()
+        multiply(3, j)
+        reduce([(k, j, s) for k in (2, 3) for s in range(subs)])
+
+    for w in both:
+        to_y[w].wait_send()
+        to_p[w].wait_send()
+        fwd[w].wait_send()
+    for k in range(n_row):
+        for j in range(chunks):
+            for s in range(subs):
+                x_copy(k, j, s).wait_send()
+                pl.when(z != owner[k])(lambda: z_copy(k, j, s, True).wait_send())
+
+
 def solution(mesh):
+    n_aux, n_row = mesh.shape["aux"], mesh.shape["row"]
+
+    def local(slabs, significant):
+        aux_here, occupied, rows = slabs.shape
+        nbf = rows * n_row
+        cols = nbf // n_aux
+        if n_row != 4 or n_aux != 2 * n_row or cols % LANES or rows % SUB or occupied % 16:
+            return plain(slabs, significant)
+        chunks = cols // LANES
+        depth = aux_here * occupied
+        mask = jnp.repeat(significant.astype(jnp.bfloat16), BS, axis=1)
+        mask = mask.reshape(aux_here, n_row, 2, chunks, LANES).transpose(1, 2, 3, 0, 4)
+        mask = jnp.broadcast_to(mask[:, :, :, :, None], (n_row, 2, chunks, aux_here, 16, LANES))
+        dma = pltpu.SemaphoreType.DMA
+        subs = rows // SUB
+        return pl.pallas_call(
+            functools.partial(kernel, n_aux, n_row, occupied),
+            out_shape=jax.ShapeDtypeStruct((rows, cols), jnp.float32),
+            in_specs=[pl.BlockSpec(memory_space=pl.ANY), pl.BlockSpec(memory_space=pltpu.VMEM)],
+            out_specs=pl.BlockSpec(memory_space=pltpu.VMEM),
+            scratch_shapes=[
+                pltpu.VMEM((n_row, chunks, 2, depth, LANES), jnp.bfloat16),
+                pltpu.VMEM((rows, depth), jnp.bfloat16),
+                pltpu.VMEM((depth, 2 * LANES), jnp.bfloat16),
+                pltpu.VMEM((n_row, chunks, 2, rows, LANES), jnp.float32),
+            ]
+            + [pltpu.VMEM((n_row, chunks, rows, LANES), jnp.float32)] * 4
+            + [dma((chunks, 2))] * 7
+            + [dma((n_row, chunks, subs))] * 5,
+            compiler_params=pltpu.CompilerParams(
+                collective_id=0, has_side_effects=True, vmem_limit_bytes=60 * 2**20
+            ),
+            cost_estimate=pl.CostEstimate(
+                flops=2 * rows * nbf * depth, bytes_accessed=2 * depth * rows, transcendentals=0
+            ),
+        )(slabs.reshape(depth, rows), mask)
+
     return jax.shard_map(
         local,
         mesh=mesh,

time: 207 us -> 107 us (0.52)
  the two profiles are of different devices: /device:TPU:19 before, /device:TPU:24 now
where the time goes in v1:
time: 107 us; the launch traced here: 106 us
  Pallas kernels  103 us (96%)
  local copies, waits for them, and re-layouts  2.95 us (3%)
    pallas_call x1, Pallas kernels, local(): pl.pallas_call(functools.partial(kernel, n_aux, n_row, occupied), out_sha...  103 us

profile of v1, /device:TPU:24, one launch (start us, length us, event | category | flops | bytes accessed | tf_op | source)
XLA Modules:
  0.0 106.4 jit_solution(11293939461736492497)
XLA Ops:
  0.0 0.7 convert_element_type.3
  0.7 0.1 broadcast_in_dim.4
  0.8 0.1 reshape_reshape.3
  0.9 0.9 broadcast_in_dim.10.mask_ref
  1.8 102.7 %shard_map.28 = f32[512,256]{1,0:T(8,128)} custom-call(bf16[3200,512]{1,0:T(8,128)(2,1)} %bitcast.3, bf16[4,2,2,8,16,128]{5,4,3,2,1,0:T(8,128)(2,1)} %broadcast_in_dim.10.mask_ref), custom_call_target="tpu_custom_call" | custom-call | flops 6710886400 | bytes 3276800 | tf_op jit(solution)/shard_map/pallas_call | solution.py:193
  104.5 1.9 %copy.5 = f32[512,256]{1,0:T(8,128)} copy(f32[512,256]{1,0:T(8,128)} %shard_map.28) | data formatting | bytes 1048576
  (1 shorter events, 0.0 us)

commit v2 on v1

--- a/solution.py
+++ b/solution.py
@@ -34,9 +34,10 @@
     return lax.psum_scatter(partial_rows, "aux", scatter_dimension=1, tiled=True)
 
 
-def kernel(n_aux, n_row, occupied, slab_hbm, mask_ref, out_ref, g, lhs_t, mk, ps, xr, zb, zlo, zhi,
-           own_sem, psend, precv, ysend, yrecv, fsend, frecv, xsend, xrecv, zsend, zlo_sem, zhi_sem):
+def kernel(n_aux, n_row, occupied, slab_hbm, mask_ref, out_ref, g, gy, lhs_t, mk, ps, xr, zb, zlo, zhi, mr,
+           own_sem, psend, precv, ysend, yrecv, fsend, frecv, xsend, xrecv, zsend, zlo_sem, zhi_sem, msend, mrecv):
     depth = slab_hbm.shape[0]
+    half = depth // 2
     chunks = g.shape[1]
     rows = ps.shape[3]
     subs = rows // SUB
@@ -58,6 +59,10 @@
     def piece(j, h):
         return slab_hbm.at[:, pl.ds(h * width + j * LANES, LANES)]
 
+    def half_piece(j, h):
+        first = pl.multiple_of((1 - y) * half, 16)
+        return slab_hbm.at[pl.ds(first, half), pl.ds(h * width + j * LANES, LANES)]
+
     def remote(src, dst, send, recv, there):
         return pltpu.make_async_remote_copy(
             src_ref=src, dst_ref=dst, send_sem=send, recv_sem=recv, device_id=there,
@@ -68,18 +73,31 @@
     own = {w: pltpu.make_async_copy(piece(*w), g.at[(0,) + w], own_sem.at[w]) for w in both}
     for w in both:
         own[w].start()
-    pl.semaphore_wait(barrier, 5)
-    to_y = {w: remote(piece(*w), g.at[(2,) + w], ysend.at[w], yrecv.at[w], {"row": across}) for w in both}
+    mirrored = z // 2 != y
+    tiles = 2 * chunks
+
+    @pl.when(mirrored)
+    def _():
+        for q in range(2):
+            pl.semaphore_signal(barrier, inc=1, device_id={"aux": r * 2 + q, "row": z},
+                                device_id_type=pl.DeviceIdType.MESH)
+
+    pl.semaphore_wait(barrier, jnp.where(mirrored, 7, 5))
+    to_y = {w: remote(half_piece(*w), gy.at[(0,) + w], ysend.at[w], yrecv.at[w], {"row": across}) for w in both}
     to_p = {w: remote(piece(*w), g.at[(1,) + w], psend.at[w], precv.at[w], {"row": partner}) for w in both}
-    fwd = {w: remote(g.at[(2,) + w], g.at[(3,) + w], fsend.at[w], frecv.at[w], {"row": partner}) for w in both}
+    fwd = {w: remote(gy.at[(0,) + w], gy.at[(1,) + w], fsend.at[w], frecv.at[w], {"row": partner}) for w in both}
     for w in both:
         to_y[w].start()
     for w in both:
         to_p[w].start()
 
     def masked(k, j, h):
-        raw = g[k, j, h].reshape(-1, occupied // 16, 16, LANES)
-        return (raw * mask_ref[owner[k], h, j][:, None]).reshape(depth, LANES)
+        if k < 2:
+            raw, mask = g[k, j, h], mask_ref[owner[k], h, j]
+        else:
+            here = half // occupied
+            raw, mask = gy[k - 2, j, h], mask_ref[owner[k], h, j, pl.ds(y * here, here)]
+        return (raw.reshape(-1, occupied // 16, 16, LANES) * mask[:, None]).reshape(raw.shape)
 
     def x_copy(k, j, s):
         part = pl.ds(s * SUB, SUB)
@@ -94,17 +112,26 @@
 
     def multiply(k, j):
         for h in range(2):
-            mk[:, h * LANES:(h + 1) * LANES] = masked(k, j, h)
+            mk[:depth if k < 2 else half, h * LANES:(h + 1) * LANES] = masked(k, j, h)
 
         @pl.loop(0, subs)
         def _(s):
             part = pl.ds(pl.multiple_of(s * SUB, SUB), SUB)
-            acc = jnp.dot(lhs_t[part, :], mk[...], preferred_element_type=jnp.float32)
+            if k < 2:
+                acc = jnp.dot(lhs_t[0, part, :], mk[:half, :], preferred_element_type=jnp.float32)
+                acc += jnp.dot(lhs_t[1, part, :], mk[half:, :], preferred_element_type=jnp.float32)
+            else:
+                acc = jnp.dot(lhs_t[y, part, :], mk[:half, :], preferred_element_type=jnp.float32)
             ps[k, j, 0, part, :] = acc[:, :LANES]
             ps[k, j, 1, part, :] = acc[:, LANES:]
 
         for s in range(subs):
             x_copy(k, j, s).start()
+
+    def m_copy(k, j, s):
+        to = x * chunks + j
+        return remote(zb.at[k, j, pl.ds(s * SUB, SUB)], mr.at[s % chunks, to], msend.at[j, s],
+                      mrecv.at[s % chunks, to], {"aux": r * 2 + s // chunks, "row": z})
 
     def sum_x(k, j, s):
         d = owner[k]
@@ -133,7 +160,10 @@
 
         @pl.when(z == d)
         def _():
-            out_ref[part, j * LANES:(j + 1) * LANES] = zb[k, j, part, :]
+            if k < 2:
+                out_ref[part, j * LANES:(j + 1) * LANES] = zb[k, j, part, :]
+            else:
+                m_copy(k, j, s).start()
 
     def reduce(jobs):
         for t in range(len(jobs) + LAG):
@@ -145,7 +175,8 @@
     for j, h in both:
         own[j, h].wait()
         mk[:, :LANES] = masked(0, j, h)
-        lhs_t[h * width + j * LANES:h * width + (j + 1) * LANES, :] = mk[:, :LANES].T
+        for e in range(2):
+            lhs_t[e, h * width + j * LANES:h * width + (j + 1) * LANES, :] = mk[e * half:(e + 1) * half, :LANES].T
     for j in range(chunks):
         multiply(0, j)
     for j in range(chunks):
@@ -162,6 +193,20 @@
             fwd[j, h].wait_recv()
         multiply(3, j)
         reduce([(k, j, s) for k in (2, 3) for s in range(subs)])
+
+    @pl.when(mirrored)
+    def _():
+        mine = jnp.where(z == across, 2, 3)
+        for first in range(chunks):
+            for s in range(first, tiles, chunks):
+                for j in range(chunks):
+                    part = pl.ds(s * SUB, SUB)
+                    remote(zb.at[mine, j, part], mr.at[j, s], msend.at[j, s], mrecv.at[j, s],
+                           {"aux": r * 2, "row": z}).wait_recv()
+                    out_ref[part, j * LANES:(j + 1) * LANES] = zb[mine, j, part, :] + mr[j, s].T
+        for j in range(chunks):
+            for s in range(tiles):
+                m_copy(mine, j, s).wait_send()
 
     for w in both:
         to_y[w].wait_send()
@@ -181,7 +226,7 @@
         aux_here, occupied, rows = slabs.shape
         nbf = rows * n_row
         cols = nbf // n_aux
-        if n_row != 4 or n_aux != 2 * n_row or cols % LANES or rows % SUB or occupied % 16:
+        if n_row != 4 or n_aux != 2 * n_row or cols % LANES or rows % SUB or occupied % 16 or aux_here % 2:
             return plain(slabs, significant)
         chunks = cols // LANES
         depth = aux_here * occupied
@@ -196,14 +241,17 @@
             in_specs=[pl.BlockSpec(memory_space=pl.ANY), pl.BlockSpec(memory_space=pltpu.VMEM)],
             out_specs=pl.BlockSpec(memory_space=pltpu.VMEM),
             scratch_shapes=[
-                pltpu.VMEM((n_row, chunks, 2, depth, LANES), jnp.bfloat16),
-                pltpu.VMEM((rows, depth), jnp.bfloat16),
+                pltpu.VMEM((2, chunks, 2, depth, LANES), jnp.bfloat16),
+                pltpu.VMEM((2, chunks, 2, depth // 2, LANES), jnp.bfloat16),
+                pltpu.VMEM((2, rows, depth // 2), jnp.bfloat16),
                 pltpu.VMEM((depth, 2 * LANES), jnp.bfloat16),
                 pltpu.VMEM((n_row, chunks, 2, rows, LANES), jnp.float32),
             ]
             + [pltpu.VMEM((n_row, chunks, rows, LANES), jnp.float32)] * 4
+            + [pltpu.VMEM((chunks, subs, SUB, LANES), jnp.float32)]
             + [dma((chunks, 2))] * 7
-            + [dma((n_row, chunks, subs))] * 5,
+            + [dma((n_row, chunks, subs))] * 5
+            + [dma((chunks, subs))] * 2,
             compiler_params=pltpu.CompilerParams(
                 collective_id=0, has_side_effects=True, vmem_limit_bytes=60 * 2**20
             ),

time: 107 us -> 104 us (0.972)
  the two profiles are of different devices: /device:TPU:24 before, /device:TPU:19 now
where the time goes in v2:
time: 104 us
  Pallas kernels  100 us (96%)
  local copies, waits for them, and re-layouts  2.95 us (3%)
    pallas_call x1, Pallas kernels, local(): pl.pallas_call(functools.partial(kernel, n_aux, n_row, occupied), out_sha...  100 us

profile of v2, /device:TPU:19, one launch (start us, length us, event | category | flops | bytes accessed | tf_op | source)
XLA Modules:
  0.0 103.7 jit_solution(13931799502546260466)
XLA Ops:
  0.0 0.7 convert_element_type.3
  0.7 0.1 broadcast_in_dim.4
  0.8 0.1 reshape_reshape.3
  0.9 0.9 broadcast_in_dim.10.mask_ref
  1.8 100.0 %shard_map.28 = f32[512,256]{1,0:T(8,128)} custom-call(bf16[3200,512]{1,0:T(8,128)(2,1)} %bitcast.3, bf16[4,2,2,8,16,128]{5,4,3,2,1,0:T(8,128)(2,1)} %broadcast_in_dim.10.mask_ref), custom_call_target="tpu_custom_call" | custom-call | flops 6710886400 | bytes 3276800 | tf_op jit(solution)/shard_map/pallas_call | solution.py:238
  101.8 1.9 %copy.5 = f32[512,256]{1,0:T(8,128)} copy(f32[512,256]{1,0:T(8,128)} %shard_map.28) | data formatting | bytes 1048576
  (1 shorter events, 0.0 us)

commit v3 on v2

--- a/solution.py
+++ b/solution.py
@@ -165,12 +165,34 @@
             else:
                 m_copy(k, j, s).start()
 
-    def reduce(jobs):
-        for t in range(len(jobs) + LAG):
-            if t < len(jobs):
-                sum_x(*jobs[t])
-            if t >= LAG:
-                sum_z(*jobs[t - LAG])
+    jobs = []
+    hops = [jnp.where(z < d, z, jnp.where(z > d, last - z, jnp.maximum(d, last - d))) for d in owner]
+
+    def sum_hops(t):
+        for hop in range(1, last + 1):
+            due = t + 1 - LAG * hop
+            if 0 <= due < len(jobs):
+                pl.when(hops[jobs[due][0]] == hop)(functools.partial(sum_z, *jobs[due]))
+
+    def reduce(k, j):
+        for s in range(subs):
+            sum_x(k, j, s)
+            jobs.append((k, j, s))
+            sum_hops(len(jobs) - 1)
+
+    def multiply_partner(j):
+        for h in range(2):
+            to_p[j, h].wait_recv()
+        multiply(1, j)
+
+    def multiply_across(j):
+        for h in range(2):
+            to_y[j, h].wait_recv()
+            fwd[j, h].start()
+        multiply(2, j)
+        for h in range(2):
+            fwd[j, h].wait_recv()
+        multiply(3, j)
 
     for j, h in both:
         own[j, h].wait()
@@ -179,20 +201,18 @@
             lhs_t[e, h * width + j * LANES:h * width + (j + 1) * LANES, :] = mk[e * half:(e + 1) * half, :LANES].T
     for j in range(chunks):
         multiply(0, j)
+    multiply_partner(0)
     for j in range(chunks):
-        for h in range(2):
-            to_p[j, h].wait_recv()
-        multiply(1, j)
-    reduce([(k, j, s) for k in range(2) for j in range(chunks) for s in range(subs)])
+        reduce(0, j)
     for j in range(chunks):
-        for h in range(2):
-            to_y[j, h].wait_recv()
-            fwd[j, h].start()
-        multiply(2, j)
-        for h in range(2):
-            fwd[j, h].wait_recv()
-        multiply(3, j)
-        reduce([(k, j, s) for k in (2, 3) for s in range(subs)])
+        multiply_across(j)
+        reduce(1, j)
+        if j + 1 < chunks:
+            multiply_partner(j + 1)
+        reduce(2, j)
+        reduce(3, j)
+    for t in range(len(jobs), len(jobs) + LAG * last):
+        sum_hops(t)
 
     @pl.when(mirrored)
     def _():

time: 104 us -> 84.6 us (0.81)
  Pallas kernels: 100 us -> 80.4 us
    pallas_call x1, Pallas kernels: 100 us -> 80.4 us  [local(): pl.pallas_call(functools.partial(kernel, n_aux, n_row, occupied), out_sha...]
where the time goes in v3:
time: 84.6 us; the launch traced here: 84.1 us
  Pallas kernels  80.4 us (95%)
  local copies, waits for them, and re-layouts  2.95 us (3%)
    pallas_call x1, Pallas kernels, local(): pl.pallas_call(functools.partial(kernel, n_aux, n_row, occupied), out_sha...  80.4 us
    unnamed x1, local copies, waits for them, and re-layouts  1.87 us

profile of v3, /device:TPU:19, one launch (start us, length us, event | category | flops | bytes accessed | tf_op | source)
XLA Modules:
  0.0 84.1 jit_solution(13697260539511152058)
XLA Ops:
  0.0 0.7 convert_element_type.3
  0.7 0.1 broadcast_in_dim.4
  0.8 0.1 reshape_reshape.3
  0.9 0.9 %broadcast_in_dim.10.mask_ref = bf16[4,2,2,8,16,128]{5,4,3,2,1,0:T(8,128)(2,1)} broadcast(bf16[4,2,2,8,128]{4,3,2,1,0:T(8,128)(2,1)S(1)} %copy.3), dimensions={0,1,2,3,5} | broadcast | bytes 557056 | tf_op jit(solution)/shard_map/broadcast_in_dim | solution.py:255
  1.8 80.4 %shard_map.28 = f32[512,256]{1,0:T(8,128)} custom-call(bf16[3200,512]{1,0:T(8,128)(2,1)} %bitcast.3, bf16[4,2,2,8,16,128]{5,4,3,2,1,0:T(8,128)(2,1)} %broadcast_in_dim.10.mask_ref), custom_call_target="tpu_custom_call" | custom-call | flops 6710886400 | bytes 3276800 | tf_op jit(solution)/shard_map/pallas_call | solution.py:258
  82.2 1.9 %copy.5 = f32[512,256]{1,0:T(8,128)} copy(f32[512,256]{1,0:T(8,128)} %shard_map.28) | data formatting | bytes 1048576
  (1 shorter events, 0.0 us)
